TPU v7x, 32 devices: a whole 2x2x4 slice. The times are simulated.
32 devices in a mesh: task: 2 (over x), ctx: 16 (over z, y, core).
Axes of the slice: x: 2, y: 2, z: 4, core: 2. Of those that a mesh axis runs over, the one named last changes fastest.
Arguments:
- base_queries: bfloat16 [2, 2048, 2048], P('task', 'ctx'), may hold values from -48 to 48
- adapter_input: bfloat16 [2, 2048, 16], P('task', 'ctx'), may hold values from -6 to 6
- adapter_up_weight: bfloat16 [2, 16, 2048], P('task'), may hold values from -1.5 to 1.5
- projected_keys: bfloat16 [2, 2048, 512], P('task', 'ctx'), may hold values from -6 to 6
- projected_values: bfloat16 [2, 2048, 512], P('task', 'ctx'), may hold values from -6 to 6
- output_gradient: bfloat16 [2, 2048, 2048], P('task', 'ctx'), may hold values from -0.52734375 to 0.52734375
- segments: int32 [2, 2048], P('task', 'ctx'), may hold values from 0 to 4, never falling along the last dimension, each value on 1 to 768 neighbouring positions
- solution: float32 [2, 32768], P('task'), may hold values from -1.5 to 1.5
- residual: float32 [2, 32768], P('task'), may hold values from -1.5 to 1.5
- direction: float32 [2, 32768], P('task'), may hold values from -1.5 to 1.5
- damping: float32 [2], P('task'), may hold values from 2 to 8
Outputs:
- new_solution: float32 [2, 32768], P('task', 'ctx')
- new_residual: float32 [2, 32768], P('task', 'ctx')
- new_direction: float32 [2, 32768], P('task', 'ctx')
- meta_gradient: float32 [32768], P('ctx')
Inputs may be any that keep to these rules, and one draw needn't show every extreme that they name: `segments`: segment numbers never fall along a task's tokens; each document holds 1 to 768 tokens, and some document holds exactly 768.
All inputs are finite; a program needn't handle non-finite values.
Results may differ from a plain program's by a relative error of at most 0.0073.
Values may be sent and summed in bfloat16 or wider, within the bound.
A program may use at most 64 MiB of HBM per device.

v0:
```python
import jax
import jax.numpy as jnp
from jax import lax
from jax.sharding import PartitionSpec as P

HEADS = 16
KV_HEADS = 4
HEAD_DIM = 128
ADAPTER_RANK = 16
SPAN = 6


def passed_along(value, axis, steps):
    count = lax.axis_size(axis)
    leading, last = (max(0, -steps), min(count, count - steps))
    return lax.ppermute(value, axis, [(source, source + steps) for source in range(leading, last)])


def attend(query_matrix, tangent_vectors, grads_in, key_window, value_window, allowed):
    per_group = HEADS // KV_HEADS
    score_scale = HEAD_DIM ** (-0.5)
    row_count = query_matrix.shape[0]
    head_parts = []
    for kv_index in range(KV_HEADS):
        low_col = kv_index * per_group * HEAD_DIM
        high_col = low_col + per_group * HEAD_DIM
        query_head = query_matrix[:, low_col:high_col].reshape(row_count, per_group, HEAD_DIM)
        tangent_head = tangent_vectors[:, low_col:high_col].reshape(row_count, per_group, HEAD_DIM)
        grad_head = grads_in[:, low_col:high_col].reshape(row_count, per_group, HEAD_DIM)
        key_head = key_window[:, kv_index * HEAD_DIM : (kv_index + 1) * HEAD_DIM]
        value_head = value_window[:, kv_index * HEAD_DIM : (kv_index + 1) * HEAD_DIM]
        scores = (
            jnp.einsum("tgd,kd->tgk", query_head, key_head, preferred_element_type=jnp.float32)
            * score_scale
        )
        slopes = (
            jnp.einsum("tgd,kd->tgk", tangent_head, key_head, preferred_element_type=jnp.float32)
            * score_scale
        )
        pulls = jnp.einsum("tgd,kd->tgk", grad_head, value_head, preferred_element_type=jnp.float32)
        key_mask = allowed[:, None, :]
        masked = jnp.where(key_mask, scores, -1e30)
        row_max = jnp.max(masked, axis=2, keepdims=True)
        exp_terms = jnp.exp(masked - row_max)
        probability = exp_terms / jnp.sum(exp_terms, axis=2, keepdims=True)
        mean_slope = jnp.sum(probability * slopes, axis=2, keepdims=True)
        mean_pull = jnp.sum(probability * pulls, axis=2, keepdims=True)
        centred = (slopes - mean_slope) * (pulls - mean_pull)
        covariance = jnp.sum(probability * centred, axis=2, keepdims=True)
        coef_rounded = (probability * (centred - covariance)).astype(jnp.bfloat16)
        head_rows = (
            jnp.einsum("tgk,kd->tgd", coef_rounded, key_head, preferred_element_type=jnp.float32)
            * score_scale
        )
        head_parts.append(head_rows.reshape(row_count, per_group * HEAD_DIM))
    return jnp.concatenate(head_parts, axis=1)


def per_device(
    base_queries,
    adapter_input,
    adapter_up_weight,
    projected_keys,
    projected_values,
    output_gradient,
    segments,
    solution,
    residual,
    direction,
    damping,
):
    tok_count = base_queries.shape[1]
    dev_index = lax.axis_index("ctx")
    adapter_rows = adapter_input[0]
    query_matrix = (
        base_queries[0].astype(jnp.float32)
        + jnp.dot(adapter_rows, adapter_up_weight[0], preferred_element_type=jnp.float32)
    ).astype(jnp.bfloat16)
    shift_matrix_fn = direction[0].reshape(ADAPTER_RANK, HEADS * HEAD_DIM)
    tangent_vectors = jnp.dot(
        adapter_rows.astype(jnp.float32), shift_matrix_fn, precision=lax.Precision.HIGHEST
    ).astype(jnp.bfloat16)
    own_block = (projected_keys[0], projected_values[0], segments[0])
    earlier = []
    for offset in range(1, SPAN + 1):
        earlier.append(passed_along((own_block[0], own_block[1], own_block[2]), "ctx", offset))
    ordered = earlier[::-1] + [own_block]
    key_window = jnp.concatenate([piece[0] for piece in ordered], axis=0)
    value_window = jnp.concatenate([piece[1] for piece in ordered], axis=0)
    seg_window = jnp.concatenate([piece[2] for piece in ordered], axis=0)
    window = (SPAN + 1) * tok_count
    key_place = dev_index * tok_count - SPAN * tok_count + jnp.arange(window, dtype=jnp.int32)
    query_place = dev_index * tok_count + jnp.arange(tok_count, dtype=jnp.int32)
    allowed = (
        (key_place[None, :] <= query_place[:, None])
        & (key_place[None, :] >= 0)
        & (seg_window[None, :] == segments[0][:, None])
    )
    curvature_product_rows = attend(
        query_matrix, tangent_vectors, output_gradient[0], key_window, value_window, allowed
    ).astype(jnp.bfloat16)
    curvature_product_term = jnp.dot(
        adapter_rows.T, curvature_product_rows, preferred_element_type=jnp.float32
    ).reshape(-1)
    damp_val = damping[0]
    dir_full = direction[0]
    res_full = residual[0]
    old_norm = jnp.sum(res_full * res_full)
    part_size = curvature_product_term.shape[0] // lax.axis_size("ctx")
    part_start = dev_index * part_size
    dir_part = lax.dynamic_slice_in_dim(dir_full, part_start, part_size, 0)
    sol_part = lax.dynamic_slice_in_dim(solution[0], part_start, part_size, 0)
    complete_curvature_product = lax.psum(curvature_product_term, "ctx")
    curved = dir_full + complete_curvature_product / damp_val
    step_len = old_norm / jnp.sum(dir_full * curved)
    res_next = res_full - step_len * curved
    ratio = jnp.sum(res_next * res_next) / old_norm
    new_residual = lax.dynamic_slice_in_dim(res_next, part_start, part_size, 0)
    new_direction = new_residual + ratio * dir_part
    new_solution = sol_part + step_len * dir_part
    meta_gradient = lax.psum(new_solution, "task") / lax.axis_size("task")
    return (new_solution[None], new_residual[None], new_direction[None], meta_gradient)


def solution(mesh):
    in_specs = (
        P("task", "ctx", None),
        P("task", "ctx", None),
        P("task", None, None),
        P("task", "ctx", None),
        P("task", "ctx", None),
        P("task", "ctx", None),
        P("task", "ctx"),
        P("task", None),
        P("task", None),
        P("task", None),
        P("task"),
    )
    out_specs = (P("task", "ctx"), P("task", "ctx"), P("task", "ctx"), P("ctx"))
    return jax.shard_map(
        per_device, mesh=mesh, in_specs=in_specs, out_specs=out_specs, check_vma=False
    )
```

profile of v0, /device:TPU:0, one launch (start us, length us, event | category | flops | bytes accessed | tf_op | source)
XLA Modules:
  0.0 246.8 jit_solution(12830081265267951997)
XLA Ops:
  7.2 6.0 %collective-permute-start = (s32[128]{0:T(128)}, s32[128]{0:T(128)S(1)}, u32[]{:S(2)}, u32[]{:S(2)}) collective-permute-start(s32[128]{0:T(128)} %bitcast.348), channel_id=1, source_target_pairs={{0,6},{1,7},{2,8},{3,9},{4,10},{5,11},{6,12},{7,13},{8,14},{9,15},... | collective-permute-start | bytes 1544 | tf_op jit(solution)/shard_map/ppermute | solution.py:16
  15.9 3.5 %collective-permute-start.2 = (s32[128]{0:T(128)}, s32[128]{0:T(128)S(1)}, u32[]{:S(2)}, u32[]{:S(2)}) collective-permute-start(s32[128]{0:T(128)} %bitcast.350), channel_id=1, source_target_pairs={{0,4},{1,5},{2,6},{3,7},{4,8},{5,9},{6,10},{7,11},{8,12},{9,13},{1... | collective-permute-start | bytes 1544 | tf_op jit(solution)/shard_map/ppermute | solution.py:16
  19.4 2.8 %collective-permute-start.3 = (s32[128]{0:T(128)}, s32[128]{0:T(128)S(1)}, u32[]{:S(2)}, u32[]{:S(2)}) collective-permute-start(s32[128]{0:T(128)} %bitcast.351), channel_id=1, source_target_pairs={{0,3},{1,4},{2,5},{3,6},{4,7},{5,8},{6,9},{7,10},{8,11},{9,12},{10... | collective-permute-start | bytes 1544 | tf_op jit(solution)/shard_map/ppermute | solution.py:16
  32.3 2.7 %collective-permute-start.6 = (bf16[128,512]{1,0:T(8,128)(2,1)S(1)}, bf16[128,512]{1,0:T(8,128)(2,1)S(1)}, u32[]{:S(2)}, u32[]{:S(2)}) collective-permute-start(bf16[128,512]{1,0:T(8,128)(2,1)S(1)} %bitcast.332), channel_id=1, source_target_pairs={{0,6},{1,7},{2,8},{3,9},{4,10},{5,11},{6,12},{7,13},{8,14},{9,15},... | collective-permute-start | bytes 393224 | tf_op jit(solution)/shard_map/ppermute | solution.py:16
  38.0 2.9 %collective-permute-start.9 = (bf16[128,512]{1,0:T(8,128)(2,1)S(1)}, bf16[128,512]{1,0:T(8,128)(2,1)S(1)}, u32[]{:S(2)}, u32[]{:S(2)}) collective-permute-start(bf16[128,512]{1,0:T(8,128)(2,1)S(1)} %bitcast.335), channel_id=1, source_target_pairs={{0,3},{1,4},{2,5},{3,6},{4,7},{5,8},{6,9},{7,10},{8,11},{9,12},{10... | collective-permute-start | bytes 393224 | tf_op jit(solution)/shard_map/ppermute | solution.py:16
  40.9 3.0 %collective-permute-start.10 = (bf16[128,512]{1,0:T(8,128)(2,1)S(1)}, bf16[128,512]{1,0:T(8,128)(2,1)S(1)}, u32[]{:S(2)}, u32[]{:S(2)}) collective-permute-start(bf16[128,512]{1,0:T(8,128)(2,1)S(1)} %bitcast.336), channel_id=1, source_target_pairs={{0,2},{1,3},{2,4},{3,5},{4,6},{5,7},{6,8},{7,9},{8,10},{9,11},{10,... | collective-permute-start | bytes 393224 | tf_op jit(solution)/shard_map/ppermute | solution.py:16
  47.9 5.4 %collective-permute-start.13 = (bf16[128,512]{1,0:T(8,128)(2,1)S(1)}, bf16[128,512]{1,0:T(8,128)(2,1)S(1)}, u32[]{:S(2)}, u32[]{:S(2)}) collective-permute-start(bf16[128,512]{1,0:T(8,128)(2,1)S(1)} %bitcast.339), channel_id=1, source_target_pairs={{0,5},{1,6},{2,7},{3,8},{4,9},{5,10},{6,11},{7,12},{8,13},{9,14},{... | collective-permute-start | bytes 393224 | tf_op jit(solution)/shard_map/ppermute | solution.py:16
  56.7 4.6 %collective-permute-start.16 = (bf16[128,512]{1,0:T(8,128)(2,1)S(1)}, bf16[128,512]{1,0:T(8,128)(2,1)S(1)}, u32[]{:S(2)}, u32[]{:S(2)}) collective-permute-start(bf16[128,512]{1,0:T(8,128)(2,1)S(1)} %bitcast.342), channel_id=1, source_target_pairs={{0,2},{1,3},{2,4},{3,5},{4,6},{5,7},{6,8},{7,9},{8,10},{9,11},{10,... | collective-permute-start | bytes 393224 | tf_op jit(solution)/shard_map/ppermute | solution.py:16
  61.4 3.5 %collective-permute-start.17 = (bf16[128,512]{1,0:T(8,128)(2,1)S(1)}, bf16[128,512]{1,0:T(8,128)(2,1)S(1)}, u32[]{:S(2)}, u32[]{:S(2)}) collective-permute-start(bf16[128,512]{1,0:T(8,128)(2,1)S(1)} %bitcast.343), channel_id=1, source_target_pairs={{0,1},{1,2},{2,3},{3,4},{4,5},{5,6},{6,7},{7,8},{8,9},{9,10},{10,1... | collective-permute-start | bytes 393224 | tf_op jit(solution)/shard_map/ppermute | solution.py:16
  65.7 3.1 %fusion.228 = (f32[128,4]{0,1:T(4,128)S(1)}, f32[128,4,896]{2,0,1:T(8,128)}) fusion(pred[128,896]{1,0:T(8,128)(4,1)S(1)} %compare_and_fusion, bf16[16,4,8,128]{3,2,1,0:T(8,128)(2,1)S(1)} %copy-done.11, bf16[896,512]{1,0:T(8,128)(2,1)} %copy-done.15), kind=kOutput, calls=%fused_computation.226 | convolution fusion | flops 119276416 | bytes 2312192 | tf_op jit(solution)/shard_map/sub | solution.py:44
  80.7 3.4 %fusion.9 = f32[128,4,896]{2,0,1:T(8,128)} fusion(bf16[128,4,128]{0,2,1:T(8,128)(2,1)S(1)} %bitcast.331, bf16[896,512]{1,0:T(8,128)(2,1)S(1)} %constant_dynamic-update-slice_fusion.8, f32[128,4,896]{2,0,1:T(8,128)} %get-tuple-element.35, f32[128,4]{0,1:T(4,128)S(1)} %get-tuple-element.34), kind=kOutput, calls=%fused_computation.9 | convolution fusion | flops 118359424 | bytes 4032512 | tf_op jit(solution)/shard_map/sub | solution.py:48
  84.0 5.7 %multiply_reduce_fusion.6 = (f32[128,4]{0,1:T(4,128)S(1)}, f32[128,4,896]{2,0,1:T(8,128)}) fusion(f32[128,4,896]{2,0,1:T(8,128)} %get-tuple-element.35, f32[128,4]{0,1:T(4,128)S(1)} %get-tuple-element.34, f32[128,4,896]{2,0,1:T(8,128)} %fusion.9, f32[896,128,4]{0,1,2:T(8,128)} %fusion.75, bf16[16,4,8,128]{3,2,1,0:T(8,128)(2,1)} %get-tuple-element.8, ...), kind=kOutput, calls=%fused_computation.46 | convolution fusion | flops 239469440 | bytes 9902080 | tf_op jit(solution)/shard_map/sub | solution.py:48
  89.7 3.8 %fusion.37 = bf16[128,4,128]{0,2,1:T(8,128)(2,1)} fusion(f32[128,4,896]{2,0,1:T(8,128)} %get-tuple-element.37, f32[128,4]{0,1:T(4,128)S(1)} %get-tuple-element.36, bf16[896,512]{1,0:T(8,128)(2,1)} %copy-done.15, f32[128,4]{0,1:T(4,128)S(1)} %get-tuple-element.34, pred[128,896]{1,0:T(8,128)(4,1)} %copy-done.13, bf16[16,4,8,128]{3,2,1,0:T(8,128)(2,1)} %get-tuple-element.12), kind=kOutput, calls=%fused_computation.63 | convolution fusion | flops 238224768 | bytes 2674688 | tf_op jit(solution)/shard_map/tgk,kd->tgd/dot_general | solution.py:52
  93.6 3.4 %fusion.6 = f32[128,4,896]{2,0,1:T(8,128)} fusion(bf16[128,4,128]{0,2,1:T(8,128)(2,1)S(1)} %bitcast.329, bf16[896,512]{1,0:T(8,128)(2,1)S(1)} %constant_dynamic-update-slice_fusion.8, f32[128,4,896]{2,0,1:T(8,128)} %get-tuple-element.31, f32[128,4]{0,1:T(4,128)S(1)} %get-tuple-element.30), kind=kOutput, calls=%fused_computation.6 | convolution fusion | flops 118359424 | bytes 4032512 | tf_op jit(solution)/shard_map/sub | solution.py:48
  96.9 5.6 %multiply_reduce_fusion.4 = (f32[128,4]{0,1:T(4,128)S(1)}, f32[128,4,896]{2,0,1:T(8,128)}) fusion(f32[128,4,896]{2,0,1:T(8,128)} %get-tuple-element.31, f32[128,4]{0,1:T(4,128)S(1)} %get-tuple-element.30, f32[128,4,896]{2,0,1:T(8,128)} %fusion.6, f32[896,128,4]{0,1,2:T(8,128)} %fusion.74, bf16[16,4,8,128]{3,2,1,0:T(8,128)(2,1)S(1)} %copy-done.12, ...), kind=kOutput, calls=%fused_computation.40 | convolution fusion | flops 239469440 | bytes 9902080 | tf_op jit(solution)/shard_map/sub | solution.py:48
  102.5 3.2 %fusion.38 = bf16[128,4,128]{0,2,1:T(8,128)(2,1)S(1)} fusion(f32[128,4,896]{2,0,1:T(8,128)} %get-tuple-element.33, f32[128,4]{0,1:T(4,128)S(1)} %get-tuple-element.32, bf16[896,512]{1,0:T(8,128)(2,1)} %copy-done.15, f32[128,4]{0,1:T(4,128)S(1)} %get-tuple-element.30, pred[128,896]{1,0:T(8,128)(4,1)} %copy-done.13, bf16[16,4,8,128]{3,2,1,0:T(8,128)(2,1)} %copy-done.9), kind=kOutput, calls=%fused_computation.64 | convolution fusion | flops 238224768 | bytes 2674688 | tf_op jit(solution)/shard_map/tgk,kd->tgd/dot_general | solution.py:52
  105.7 3.4 %fusion.3 = f32[128,4,896]{2,0,1:T(8,128)} fusion(bf16[128,4,128]{0,2,1:T(8,128)(2,1)S(1)} %bitcast.327, bf16[896,512]{1,0:T(8,128)(2,1)S(1)} %constant_dynamic-update-slice_fusion.8, f32[128,4,896]{2,0,1:T(8,128)} %get-tuple-element.27, f32[128,4]{0,1:T(4,128)S(1)} %get-tuple-element.26), kind=kOutput, calls=%fused_computation.3 | convolution fusion | flops 118359424 | bytes 4032512 | tf_op jit(solution)/shard_map/sub | solution.py:48
  109.1 5.8 %multiply_reduce_fusion.2 = (f32[128,4]{0,1:T(4,128)S(1)}, f32[128,4,896]{2,0,1:T(8,128)}) fusion(f32[128,4,896]{2,0,1:T(8,128)} %get-tuple-element.27, f32[128,4]{0,1:T(4,128)S(1)} %get-tuple-element.26, f32[128,4,896]{2,0,1:T(8,128)} %fusion.3, f32[896,128,4]{0,1,2:T(8,128)} %fusion.73, bf16[16,4,8,128]{3,2,1,0:T(8,128)(2,1)S(1)} %copy-done.10, ...), kind=kOutput, calls=%fused_computation.34 | convolution fusion | flops 239469440 | bytes 9902080 | tf_op jit(solution)/shard_map/sub | solution.py:48
  115.0 3.2 %fusion.39 = bf16[128,4,128]{0,2,1:T(8,128)(2,1)S(1)} fusion(f32[128,4,896]{2,0,1:T(8,128)} %get-tuple-element.29, f32[128,4]{0,1:T(4,128)S(1)} %get-tuple-element.28, bf16[896,512]{1,0:T(8,128)(2,1)} %copy-done.15, f32[128,4]{0,1:T(4,128)S(1)} %get-tuple-element.26, pred[128,896]{1,0:T(8,128)(4,1)} %copy-done.13, bf16[16,4,8,128]{3,2,1,0:T(8,128)(2,1)} %copy-done.7), kind=kOutput, calls=%fused_computation.65 | convolution fusion | flops 238224768 | bytes 2674688 | tf_op jit(solution)/shard_map/tgk,kd->tgd/dot_general | solution.py:52
  118.2 3.3 %fusion = f32[128,4,896]{2,0,1:T(8,128)} fusion(bf16[128,4,128]{0,2,1:T(8,128)(2,1)S(1)} %bitcast.325, bf16[896,512]{1,0:T(8,128)(2,1)S(1)} %constant_dynamic-update-slice_fusion.8, f32[128,4,896]{2,0,1:T(8,128)} %get-tuple-element.23, f32[128,4]{0,1:T(4,128)S(1)} %get-tuple-element.22), kind=kOutput, calls=%fused_computation | convolution fusion | flops 118359424 | bytes 4032512 | tf_op jit(solution)/shard_map/sub | solution.py:48
  121.5 5.1 %multiply_reduce_fusion = (f32[128,4]{0,1:T(4,128)S(1)}, f32[128,4,896]{2,0,1:T(8,128)}) fusion(f32[128,4,896]{2,0,1:T(8,128)} %get-tuple-element.23, f32[128,4]{0,1:T(4,128)S(1)} %get-tuple-element.22, f32[128,4,896]{2,0,1:T(8,128)} %fusion, f32[896,128,4]{0,1,2:T(8,128)S(1)} %fusion.72, bf16[16,4,8,128]{3,2,1,0:T(8,128)(2,1)S(1)} %copy-done.8, ...), kind=kOutput, calls=%fused_computation.28 | convolution fusion | flops 239469440 | bytes 9902080 | tf_op jit(solution)/shard_map/sub | solution.py:48
  126.6 3.2 %fusion.40 = bf16[128,4,128]{0,2,1:T(8,128)(2,1)S(1)} fusion(f32[128,4,896]{2,0,1:T(8,128)} %get-tuple-element.25, f32[128,4]{0,1:T(4,128)S(1)} %get-tuple-element.24, bf16[896,512]{1,0:T(8,128)(2,1)S(1)} %copy-done.17, f32[128,4]{0,1:T(4,128)S(1)} %get-tuple-element.22, pred[128,896]{1,0:T(8,128)(4,1)} %copy-done.13, bf16[16,4,8,128]{3,2,1,0:T(8,128)(2,1)} %copy-done.6), kind=kOutput, calls=%fused_computation.66 | convolution fusion | flops 238224768 | bytes 2674688 | tf_op jit(solution)/shard_map/tgk,kd->tgd/dot_general | solution.py:52
  131.4 95.8 %all-reduce.2.cloned.1.call-done = f32[32768]{0:T(1024)} async-done(((f32[32768]{0:T(1024)}), f32[32768]{0:T(1024)}) %all-reduce.2.cloned.1.call-update) | async-done | bytes 131088 | tf_op jit(solution)/shard_map/psum | solution.py:113
  233.7 5.0 %psum.15 = f32[2048]{0:T(1024)S(1)} all-reduce(f32[2048]{0:T(1024)S(1)} %bitcast.344), channel_id=1, replica_groups=mesh['task'=2,'ctx'=16] {'task'}, use_global_device_ids=true, to_apply=%region_24.25 | all-reduce | flops 2048 | bytes 16384 | tf_op jit(solution)/shard_map/psum | solution.py:121
  (121 shorter events, 41.3 us)
Async XLA Ops:
  7.2 220.0 %all-reduce.2.cloned.1.call-start = ((), (), s32[]{:S(2)}) async-start(), calls=%async_computation | async-start | bytes 262144 | tf_op jit(solution)/shard_map/psum | solution.py:113
  7.2 23.3 %collective-permute-start = (s32[128]{0:T(128)}, s32[128]{0:T(128)S(1)}, u32[]{:S(2)}, u32[]{:S(2)}) collective-permute-start(s32[128]{0:T(128)} %bitcast.348), channel_id=1, source_target_pairs={{0,6},{1,7},{2,8},{3,9},{4,10},{5,11},{6,12},{7,13},{8,14},{9,15},... | collective-permute-start | bytes 1544 | tf_op jit(solution)/shard_map/ppermute | solution.py:16
  13.3 19.0 %collective-permute-start.1 = (s32[128]{0:T(128)}, s32[128]{0:T(128)S(1)}, u32[]{:S(2)}, u32[]{:S(2)}) collective-permute-start(s32[128]{0:T(128)} %bitcast.349), channel_id=1, source_target_pairs={{0,5},{1,6},{2,7},{3,8},{4,9},{5,10},{6,11},{7,12},{8,13},{9,14},{... | collective-permute-start | bytes 1544 | tf_op jit(solution)/shard_map/ppermute | solution.py:16
  15.9 19.1 %collective-permute-start.2 = (s32[128]{0:T(128)}, s32[128]{0:T(128)S(1)}, u32[]{:S(2)}, u32[]{:S(2)}) collective-permute-start(s32[128]{0:T(128)} %bitcast.350), channel_id=1, source_target_pairs={{0,4},{1,5},{2,6},{3,7},{4,8},{5,9},{6,10},{7,11},{8,12},{9,13},{1... | collective-permute-start | bytes 1544 | tf_op jit(solution)/shard_map/ppermute | solution.py:16
  19.4 17.2 %collective-permute-start.3 = (s32[128]{0:T(128)}, s32[128]{0:T(128)S(1)}, u32[]{:S(2)}, u32[]{:S(2)}) collective-permute-start(s32[128]{0:T(128)} %bitcast.351), channel_id=1, source_target_pairs={{0,3},{1,4},{2,5},{3,6},{4,7},{5,8},{6,9},{7,10},{8,11},{9,12},{10... | collective-permute-start | bytes 1544 | tf_op jit(solution)/shard_map/ppermute | solution.py:16
  22.2 15.8 %collective-permute-start.4 = (s32[128]{0:T(128)}, s32[128]{0:T(128)S(1)}, u32[]{:S(2)}, u32[]{:S(2)}) collective-permute-start(s32[128]{0:T(128)} %bitcast.352), channel_id=1, source_target_pairs={{0,2},{1,3},{2,4},{3,5},{4,6},{5,7},{6,8},{7,9},{8,10},{9,11},{10,... | collective-permute-start | bytes 1544 | tf_op jit(solution)/shard_map/ppermute | solution.py:16
  26.6 42.2 %copy-start.9 = (bf16[16,4,8,128]{3,2,1,0:T(8,128)(2,1)}, bf16[16,4,8,128]{3,2,1,0:T(8,128)(2,1)S(1)}, u32[]{:S(2)}) copy-start(bf16[16,4,8,128]{3,2,1,0:T(8,128)(2,1)S(1)} %get-tuple-element.15) | copy-start | bytes 393220
  26.6 47.8 %copy-start.7 = (bf16[16,4,8,128]{3,2,1,0:T(8,128)(2,1)}, bf16[16,4,8,128]{3,2,1,0:T(8,128)(2,1)S(1)}, u32[]{:S(2)}) copy-start(bf16[16,4,8,128]{3,2,1,0:T(8,128)(2,1)S(1)} %get-tuple-element.14) | copy-start | bytes 393220
  26.6 51.5 %copy-start.6 = (bf16[16,4,8,128]{3,2,1,0:T(8,128)(2,1)}, bf16[16,4,8,128]{3,2,1,0:T(8,128)(2,1)S(1)}, u32[]{:S(2)}) copy-start(bf16[16,4,8,128]{3,2,1,0:T(8,128)(2,1)S(1)} %get-tuple-element.13) | copy-start | bytes 393220
  30.6 10.3 %collective-permute-start.5 = (s32[128]{0:T(128)S(1)}, s32[128]{0:T(128)S(1)}, u32[]{:S(2)}, u32[]{:S(2)}) collective-permute-start(s32[128]{0:T(128)S(1)} %bitcast.353), channel_id=1, source_target_pairs={{0,1},{1,2},{2,3},{3,4},{4,5},{5,6},{6,7},{7,8},{8,9},{9,10},{10,1... | collective-permute-start | bytes 1544 | tf_op jit(solution)/shard_map/ppermute | solution.py:16
  32.3 11.9 %collective-permute-start.6 = (bf16[128,512]{1,0:T(8,128)(2,1)S(1)}, bf16[128,512]{1,0:T(8,128)(2,1)S(1)}, u32[]{:S(2)}, u32[]{:S(2)}) collective-permute-start(bf16[128,512]{1,0:T(8,128)(2,1)S(1)} %bitcast.332), channel_id=1, source_target_pairs={{0,6},{1,7},{2,8},{3,9},{4,10},{5,11},{6,12},{7,13},{8,14},{9,15},... | collective-permute-start | bytes 393224 | tf_op jit(solution)/shard_map/ppermute | solution.py:16
  35.1 10.6 %collective-permute-start.7 = (bf16[128,512]{1,0:T(8,128)(2,1)S(1)}, bf16[128,512]{1,0:T(8,128)(2,1)S(1)}, u32[]{:S(2)}, u32[]{:S(2)}) collective-permute-start(bf16[128,512]{1,0:T(8,128)(2,1)S(1)} %bitcast.333), channel_id=1, source_target_pairs={{0,5},{1,6},{2,7},{3,8},{4,9},{5,10},{6,11},{7,12},{8,13},{9,14},{... | collective-permute-start | bytes 393224 | tf_op jit(solution)/shard_map/ppermute | solution.py:16
  36.7 11.3 %collective-permute-start.8 = (bf16[128,512]{1,0:T(8,128)(2,1)S(1)}, bf16[128,512]{1,0:T(8,128)(2,1)S(1)}, u32[]{:S(2)}, u32[]{:S(2)}) collective-permute-start(bf16[128,512]{1,0:T(8,128)(2,1)S(1)} %bitcast.334), channel_id=1, source_target_pairs={{0,4},{1,5},{2,6},{3,7},{4,8},{5,9},{6,10},{7,11},{8,12},{9,13},{1... | collective-permute-start | bytes 393224 | tf_op jit(solution)/shard_map/ppermute | solution.py:16
  38.0 15.4 %collective-permute-start.9 = (bf16[128,512]{1,0:T(8,128)(2,1)S(1)}, bf16[128,512]{1,0:T(8,128)(2,1)S(1)}, u32[]{:S(2)}, u32[]{:S(2)}) collective-permute-start(bf16[128,512]{1,0:T(8,128)(2,1)S(1)} %bitcast.335), channel_id=1, source_target_pairs={{0,3},{1,4},{2,5},{3,6},{4,7},{5,8},{6,9},{7,10},{8,11},{9,12},{10... | collective-permute-start | bytes 393224 | tf_op jit(solution)/shard_map/ppermute | solution.py:16
  40.9 13.8 %collective-permute-start.10 = (bf16[128,512]{1,0:T(8,128)(2,1)S(1)}, bf16[128,512]{1,0:T(8,128)(2,1)S(1)}, u32[]{:S(2)}, u32[]{:S(2)}) collective-permute-start(bf16[128,512]{1,0:T(8,128)(2,1)S(1)} %bitcast.336), channel_id=1, source_target_pairs={{0,2},{1,3},{2,4},{3,5},{4,6},{5,7},{6,8},{7,9},{8,10},{9,11},{10,... | collective-permute-start | bytes 393224 | tf_op jit(solution)/shard_map/ppermute | solution.py:16
  44.2 34.0 %copy-start.13 = (pred[128,896]{1,0:T(8,128)(4,1)}, pred[128,896]{1,0:T(8,128)(4,1)S(1)}, u32[]{:S(2)}) copy-start(pred[128,896]{1,0:T(8,128)(4,1)S(1)} %compare_and_fusion) | copy-start | bytes 344068
  44.2 21.5 %copy-start.11 = (bf16[16,4,8,128]{3,2,1,0:T(8,128)(2,1)S(1)}, bf16[16,4,8,128]{3,2,1,0:T(8,128)(2,1)}, u32[]{:S(2)}) copy-start(bf16[16,4,8,128]{3,2,1,0:T(8,128)(2,1)} %get-tuple-element.12) | copy-start | bytes 393220
  44.2 12.5 %collective-permute-start.11 = (bf16[128,512]{1,0:T(8,128)(2,1)S(1)}, bf16[128,512]{1,0:T(8,128)(2,1)S(1)}, u32[]{:S(2)}, u32[]{:S(2)}) collective-permute-start(bf16[128,512]{1,0:T(8,128)(2,1)S(1)} %bitcast.337), channel_id=1, source_target_pairs={{0,1},{1,2},{2,3},{3,4},{4,5},{5,6},{6,7},{7,8},{8,9},{9,10},{10,1... | collective-permute-start | bytes 393224 | tf_op jit(solution)/shard_map/ppermute | solution.py:16
  45.7 15.7 %collective-permute-start.12 = (bf16[128,512]{1,0:T(8,128)(2,1)S(1)}, bf16[128,512]{1,0:T(8,128)(2,1)S(1)}, u32[]{:S(2)}, u32[]{:S(2)}) collective-permute-start(bf16[128,512]{1,0:T(8,128)(2,1)S(1)} %bitcast.338), channel_id=1, source_target_pairs={{0,6},{1,7},{2,8},{3,9},{4,10},{5,11},{6,12},{7,13},{8,14},{9,15},... | collective-permute-start | bytes 393224 | tf_op jit(solution)/shard_map/ppermute | solution.py:16
  47.9 17.0 %collective-permute-start.13 = (bf16[128,512]{1,0:T(8,128)(2,1)S(1)}, bf16[128,512]{1,0:T(8,128)(2,1)S(1)}, u32[]{:S(2)}, u32[]{:S(2)}) collective-permute-start(bf16[128,512]{1,0:T(8,128)(2,1)S(1)} %bitcast.339), channel_id=1, source_target_pairs={{0,5},{1,6},{2,7},{3,8},{4,9},{5,10},{6,11},{7,12},{8,13},{9,14},{... | collective-permute-start | bytes 393224 | tf_op jit(solution)/shard_map/ppermute | solution.py:16
  53.4 11.5 %collective-permute-start.14 = (bf16[128,512]{1,0:T(8,128)(2,1)S(1)}, bf16[128,512]{1,0:T(8,128)(2,1)S(1)}, u32[]{:S(2)}, u32[]{:S(2)}) collective-permute-start(bf16[128,512]{1,0:T(8,128)(2,1)S(1)} %bitcast.340), channel_id=1, source_target_pairs={{0,4},{1,5},{2,6},{3,7},{4,8},{5,9},{6,10},{7,11},{8,12},{9,13},{1... | collective-permute-start | bytes 393224 | tf_op jit(solution)/shard_map/ppermute | solution.py:16
  54.8 10.2 %collective-permute-start.15 = (bf16[128,512]{1,0:T(8,128)(2,1)S(1)}, bf16[128,512]{1,0:T(8,128)(2,1)S(1)}, u32[]{:S(2)}, u32[]{:S(2)}) collective-permute-start(bf16[128,512]{1,0:T(8,128)(2,1)S(1)} %bitcast.341), channel_id=1, source_target_pairs={{0,3},{1,4},{2,5},{3,6},{4,7},{5,8},{6,9},{7,10},{8,11},{9,12},{10... | collective-permute-start | bytes 393224 | tf_op jit(solution)/shard_map/ppermute | solution.py:16
  56.7 8.3 %collective-permute-start.16 = (bf16[128,512]{1,0:T(8,128)(2,1)S(1)}, bf16[128,512]{1,0:T(8,128)(2,1)S(1)}, u32[]{:S(2)}, u32[]{:S(2)}) collective-permute-start(bf16[128,512]{1,0:T(8,128)(2,1)S(1)} %bitcast.342), channel_id=1, source_target_pairs={{0,2},{1,3},{2,4},{3,5},{4,6},{5,7},{6,8},{7,9},{8,10},{9,11},{10,... | collective-permute-start | bytes 393224 | tf_op jit(solution)/shard_map/ppermute | solution.py:16
  61.4 4.3 %collective-permute-start.17 = (bf16[128,512]{1,0:T(8,128)(2,1)S(1)}, bf16[128,512]{1,0:T(8,128)(2,1)S(1)}, u32[]{:S(2)}, u32[]{:S(2)}) collective-permute-start(bf16[128,512]{1,0:T(8,128)(2,1)S(1)} %bitcast.343), channel_id=1, source_target_pairs={{0,1},{1,2},{2,3},{3,4},{4,5},{5,6},{6,7},{7,8},{8,9},{9,10},{10,1... | collective-permute-start | bytes 393224 | tf_op jit(solution)/shard_map/ppermute | solution.py:16
  (16 other events, 101.9 us)
Sparse Core Ops, SparseCore 0:
  130.9 96.2 all-reduce.1
where the time goes:
time: 249 us; the launch traced here: 247 us
  waiting for transfers between devices  96.5 us (39%)
  matrix products  66.2 us (27%)
  starting transfers between devices  50.8 us (20%)
  between operations  18.1 us (7%)
  other arithmetic  6.81 us (3%)
  blocking collectives  5 us (2%)
  local copies, waits for them, and re-layouts  3.33 us (1%)
    psum x1, waiting for transfers between devices, per_device(): complete_curvature_product = lax.psum(curvature_product_term, 'ctx')  95.8 us
    ppermute x18, starting transfers between devices, passed_along(): lax.ppermute(value, axis, [(source, source + steps) for source in range(l...  50.8 us
    sub x8, matrix products, attend(): centred = (slopes - mean_slope) * (pulls - mean_pull)  35.7 us
    dot_general x4, matrix products, attend(): jnp.einsum('tgk,kd->tgd', coef_rounded, key_head, preferred_element_type=...  13.3 us
    sub x4, matrix products, attend(): exp_terms = jnp.exp(masked - row_max)  9.35 us
    dot_general x4, matrix products, attend(): jnp.einsum('tgd,kd->tgk', grad_head, value_head, preferred_element_type=j...  5.59 us
    psum x1, blocking collectives, per_device(): meta_gradient = lax.psum(new_solution, 'task') / lax.axis_size('task')  5 us
  transfers between devices with their start and end apart: 19, of which 2 were waited for; matrix products, arithmetic and copies ran while one was open for 3% of the time, Pallas kernels for 0%

commit v1 on v0

v1 whole, which is shorter than its diff:
```python
import functools

import jax
import jax.numpy as jnp
from jax import lax
from jax.experimental import pallas as pl
from jax.experimental.pallas import tpu as pltpu
from jax.sharding import PartitionSpec as P

KV_HEADS = 4
HEAD_DIM = 128
SPAN = 6
LANES = 128
MESH = pl.DeviceIdType.MESH
NT = (((1,), (1,)), ((), ()))


def kernel(
    dims,
    base_ref, ain_ref, up_ref, key_ref, val_ref, grad_ref, seg_ref,
    sol_ref, res_ref, dir_ref, dirmat_ref, damp_ref,
    nsol_ref, nres_ref, ndir_ref, meta_ref,
    kbuf, vbuf, segbuf, qin, gin, ain, qs, ts, gs, dsel,
    sbuf, tbuf, ubuf, mbuf, cbuf, hvacc, hvsend, hvrecv, dhsend, dhrecv,
    nrsend, nrrecv, solrecv,
    own_send, sib_send, sib_recv, seg_send, seg_recv, k_recv, v_recv, relay_send,
    hv_ssem, hv_rsem, dh_ssem, dh_rsem, nr_ssem, nr_rsem, sol_ssem, sol_rsem,
):
    tasks, ctx, rank, heads, part_rows, piece, nq = dims
    chips = ctx // 2
    per = heads // KV_HEADS
    tok = base_ref.shape[0]
    half = heads * HEAD_DIM // 2
    khalf = key_ref.shape[1] // 2
    hloc = heads // 2
    kvloc = KV_HEADS // 2
    nwin = SPAN + 2
    win = SPAN + 1
    back = SPAN // 2
    wide = per * tok
    f32, bf16 = jnp.float32, jnp.bfloat16
    me_t = lax.axis_index("task")
    me = lax.axis_index("ctx")
    c = me // 2
    k = lax.rem(me, 2)
    odd = lax.rem(c, 2)
    sib = me + 1 - 2 * k

    def dev(n):
        return (me_t, n)

    barrier = pltpu.get_barrier_semaphore()

    def greet(i, carry):
        pl.semaphore_signal(barrier, inc=1, device_id=dev(lax.rem(me + i, ctx)), device_id_type=MESH)
        return carry

    lax.fori_loop(1, ctx, greet, 0)
    for i in range(1, tasks):
        pl.semaphore_signal(barrier, inc=1, device_id=(lax.rem(me_t + i, tasks), me), device_id_type=MESH)
    pl.semaphore_wait(barrier, ctx - 1 + tasks - 1)

    def rc(src, dst, ssem, rsem, n):
        return pltpu.make_async_remote_copy(
            src_ref=src, dst_ref=dst, send_sem=ssem, recv_sem=rsem, device_id=dev(n), device_id_type=MESH
        )

    def kcols(h):
        return pl.ds(pl.multiple_of(h * khalf, LANES), khalf)

    def qcols(h):
        return pl.ds(pl.multiple_of(h * half, LANES), half)

    other = 1 - k
    sib_copies = [
        rc(ain_ref, ain.at[k], sib_send.at[0], sib_recv.at[0], sib),
        rc(base_ref.at[:, qcols(other)], qin.at[k], sib_send.at[1], sib_recv.at[1], sib),
        rc(grad_ref.at[:, qcols(other)], gin.at[k], sib_send.at[2], sib_recv.at[2], sib),
        rc(key_ref.at[:, kcols(other)], kbuf.at[SPAN + k], sib_send.at[3], k_recv.at[SPAN + k], sib),
        rc(val_ref.at[:, kcols(other)], vbuf.at[SPAN + k], sib_send.at[4], v_recv.at[SPAN + k], sib),
    ]
    ahead2, ahead1 = [], []
    for h in range(2):
        for copies, d in ((ahead2, 2), (ahead1, 1)):
            n = 2 * (c + d) + h
            w = SPAN - 2 * d + k
            s = 4 * (d - 1) + 2 * h
            copies.append(rc(key_ref.at[:, kcols(h)], kbuf.at[w], own_send.at[s], k_recv.at[w], n))
            copies.append(rc(val_ref.at[:, kcols(h)], vbuf.at[w], own_send.at[s + 1], v_recv.at[w], n))
    seg_copies = []
    for d in range(back + 1):
        for h in range(2):
            w = SPAN - 2 * d + k
            n = 2 * (c + d) + h
            seg_copies.append((d, h, rc(seg_ref, segbuf.at[w], seg_send.at[2 * d + h], seg_recv.at[w], n)))
    go2 = c + 2 < chips
    go1 = odd == 0

    def start_all(copies):
        for copy in copies:
            copy.start()

    pl.when(go2)(lambda: start_all(ahead2))
    pl.when(go1)(lambda: start_all(ahead1))
    start_all(sib_copies)
    for d, h, copy in seg_copies:
        ok = (c + d < chips) if d else (k != h)
        pl.when(ok)(copy.start)

    for w in range(SPAN):
        @pl.when(c < back - w // 2)
        def _(w=w):
            kbuf[w] = jnp.zeros(kbuf.shape[1:], bf16)
            vbuf[w] = jnp.zeros(vbuf.shape[1:], bf16)
            segbuf[w] = jnp.full(segbuf.shape[1:], -1, jnp.int32)

    for s in range(2):
        @pl.when(k == s)
        def _(s=s):
            kbuf[SPAN + s] = key_ref[:, s * khalf:(s + 1) * khalf]
            vbuf[SPAN + s] = val_ref[:, s * khalf:(s + 1) * khalf]
            segbuf[SPAN + s] = seg_ref[...]
            qin[s] = base_ref[:, s * half:(s + 1) * half]
            gin[s] = grad_ref[:, s * half:(s + 1) * half]
            ain[s] = ain_ref[...]

    first = k == 0
    up = jnp.where(first, up_ref[:, :half].astype(f32), up_ref[:, half:].astype(f32)).astype(bf16)
    for j in range(hloc):
        dsel[j] = jnp.where(first, dirmat_ref[:, j, :], dirmat_ref[:, hloc + j, :])
    dmat = jnp.concatenate([dsel[j] for j in range(hloc)], axis=1)
    d1 = dmat.astype(bf16)
    rest = dmat - d1.astype(f32)
    d2 = rest.astype(bf16)
    d3 = (rest - d2.astype(f32)).astype(bf16)
    old_norm = jnp.sum(jnp.sum(res_ref[...] * res_ref[...], axis=0), keepdims=True)
    dir_norm = jnp.sum(jnp.sum(dir_ref[...] * dir_ref[...], axis=0), keepdims=True)
    mbuf[...] = jnp.full(mbuf.shape, -1e30, f32)

    def recv(buf, sem):
        rc(buf, buf, relay_send.at[0], sem, sib).wait_recv()

    recv(ain.at[other], sib_recv.at[0])
    recv(qin.at[other], sib_recv.at[1])
    recv(gin.at[other], sib_recv.at[2])
    recv(segbuf.at[SPAN + other], seg_recv.at[SPAN + other])
    recv(kbuf.at[SPAN + other], k_recv.at[SPAN + other])
    recv(vbuf.at[SPAN + other], v_recv.at[SPAN + other])

    for qb in range(2):
        a = ain[qb]
        lora = jnp.dot(a, up, preferred_element_type=f32)
        tan = (
            jnp.dot(a, d1, preferred_element_type=f32)
            + jnp.dot(a, d2, preferred_element_type=f32)
            + jnp.dot(a, d3, preferred_element_type=f32)
        ).astype(bf16)
        que = (qin[qb].astype(f32) + lora).astype(bf16)
        for j in range(hloc):
            h, g = j // per, j % per
            cols = slice(j * HEAD_DIM, (j + 1) * HEAD_DIM)
            rows = slice(g * tok, (g + 1) * tok)
            qs[qb, h, rows] = que[:, cols]
            ts[qb, h, rows] = tan[:, cols]
            gs[qb, h, rows] = gin[qb, :, cols]

    def stage(d):
        for s in range(2):
            w = SPAN - 2 * d + s
            seg_k = jnp.broadcast_to(segbuf[w], (tok, tok)).T
            for qb in range(2):
                if not qb <= w <= qb + SPAN:
                    continue
                allowed = seg_k == jnp.broadcast_to(segbuf[SPAN + qb], (tok, tok))
                if w == qb + SPAN:
                    allowed &= lax.broadcasted_iota(jnp.int32, (tok, tok), 0) <= lax.broadcasted_iota(
                        jnp.int32, (tok, tok), 1
                    )
                bias = jnp.where(allowed, 0.0, -1e30)
                for h in range(kvloc):
                    kb = kbuf[w, :, h * HEAD_DIM:(h + 1) * HEAD_DIM]
                    vb = vbuf[w, :, h * HEAD_DIM:(h + 1) * HEAD_DIM]
                    sc = lax.dot_general(kb, qs[qb, h], NT, preferred_element_type=f32)
                    for g in range(per):
                        cols = slice(g * tok, (g + 1) * tok)
                        part = sc[:, cols] + bias
                        sbuf[qb, h, w, :, cols] = part
                        top = jnp.max(part.reshape(tok // 8, 8, tok), axis=0)
                        mbuf[qb, h, :, cols] = jnp.maximum(mbuf[qb, h, :, cols], top)
                    tbuf[qb, h, w] = lax.dot_general(kb, ts[qb, h], NT, preferred_element_type=f32)
                    ubuf[qb, h, w] = lax.dot_general(vb, gs[qb, h], NT, preferred_element_type=f32)

    relay3, relay1 = [], []
    for s in range(2):
        w = SPAN - 4 + s
        n = 2 * (c - 1) + k
        relay1.append(rc(kbuf.at[w], kbuf.at[w + 2], relay_send.at[2 * s], k_recv.at[w + 2], n))
        relay1.append(rc(vbuf.at[w], vbuf.at[w + 2], relay_send.at[2 * s + 1], v_recv.at[w + 2], n))
    for s in range(2):
        w = SPAN - 2 + s
        n = 2 * (c + 2) + k
        relay3.append(rc(kbuf.at[w], kbuf.at[w - 4], relay_send.at[4 + 2 * s], k_recv.at[w - 4], n))
        relay3.append(rc(vbuf.at[w], vbuf.at[w - 4], relay_send.at[5 + 2 * s], v_recv.at[w - 4], n))

    def arrive(d, relays, cond):
        @pl.when(c >= d)
        def _():
            for s in range(2):
                w = SPAN - 2 * d + s
                recv(kbuf.at[w], k_recv.at[w])
                if relays:
                    pl.when(cond)(relays[2 * s].start)
                recv(vbuf.at[w], v_recv.at[w])
                if relays:
                    pl.when(cond)(relays[2 * s + 1].start)
            for s in range(2):
                w = SPAN - 2 * d + s
                recv(segbuf.at[w], seg_recv.at[w])

    stage(0)
    arrive(2, relay1, odd == 1)
    arrive(1, relay3, go2)
    stage(2)
    stage(1)
    arrive(3, [], None)
    stage(3)

    factor = HEAD_DIM ** -0.5 * 1.4426950408889634
    nblk = tok // 8
    for qb in range(2):
        at_ = ain[qb].astype(f32).T
        for h in range(kvloc):
            rows_of = []
            for g in range(per):
                cols = slice(g * tok, (g + 1) * tok)
                top = jnp.max(mbuf[qb, h, :, cols], axis=0, keepdims=True)

                def moments(w, acc, cols=cols, top=top, qb=qb, h=h):
                    e = jnp.exp2((sbuf[qb, h, qb + w, :, cols] - top) * factor)
                    sbuf[qb, h, qb + w, :, cols] = e
                    t = tbuf[qb, h, qb + w, :, cols]
                    u = ubuf[qb, h, qb + w, :, cols]
                    et = e * t

                    def fold(x):
                        return jnp.sum(x.reshape(nblk, 8, tok), axis=0)

                    return (acc[0] + fold(e), acc[1] + fold(et), acc[2] + fold(e * u), acc[3] + fold(et * u))

                zero = jnp.zeros((8, tok), f32)
                z, st, su, stu = lax.fori_loop(0, win, moments, (zero, zero, zero, zero))
                z, st, su, stu = (jnp.sum(x, axis=0, keepdims=True) for x in (z, st, su, stu))
                rz = 1.0 / z
                mt, mu = st * rz, su * rz
                cov = stu * rz - mt * mu

                def coefs(w, carry, cols=cols, mt=mt, mu=mu, cov=cov, qb=qb, h=h):
                    e = sbuf[qb, h, qb + w, :, cols]
                    t = tbuf[qb, h, qb + w, :, cols]
                    u = ubuf[qb, h, qb + w, :, cols]
                    cbuf[qb, h, w, :, cols] = (e * ((t - mt) * (u - mu) - cov)).astype(bf16)
                    return carry

                lax.fori_loop(0, win, coefs, 0)
                az = (at_ * rz).astype(bf16)
                cw = cbuf[qb, h, :, :, cols].reshape(win * tok, tok)
                rows_of.append(lax.dot_general(az, cw, NT, preferred_element_type=f32).astype(bf16))
            kw = kbuf[qb:qb + win, :, h * HEAD_DIM:(h + 1) * HEAD_DIM].reshape(win * tok, HEAD_DIM)
            hv = jnp.dot(jnp.concatenate(rows_of, axis=0), kw, preferred_element_type=f32)
            if qb == 0:
                hvacc[h] = hv
            else:
                hvacc[h] = (hvacc[h] + hv) * (1.0 / HEAD_DIM)

    dh = jnp.zeros((rank, LANES), f32)
    for j in range(hloc):
        h, g = j // per, j % per
        hv = hvacc[h, g * rank:(g + 1) * rank]
        hvsend[:, j // piece, j % piece, :] = hv
        dh = dh + hv * dsel[j]
    dh = jnp.sum(dh.reshape(rank // 8, 8, LANES), axis=0)
    dhsend[...] = dh
    dhrecv[me] = dh

    row0 = k * hloc
    groups = part_rows // piece

    def hv_copy(i):
        r, q = i // nq, lax.rem(i, nq)
        flat = r * heads + row0 + q * piece
        owner = flat // part_rows
        slot = c * groups + lax.rem(flat, part_rows) // piece
        return r, q, owner, slot, rc(hvsend.at[r, q], hvrecv.at[slot], hv_ssem.at[i], hv_rsem.at[slot], owner)

    def hv_start(i, carry):
        r, q, owner, slot, copy = hv_copy(i)
        pl.when(owner != me)(copy.start)

        @pl.when(owner == me)
        def _():
            hvrecv[slot] = hvsend[r, q]

        return carry

    lax.fori_loop(0, rank * nq, hv_start, 0)

    def dh_copy(i):
        return rc(dhsend, dhrecv.at[me], dh_ssem.at[i], dh_rsem.at[me], lax.rem(me + i, ctx))

    def each(lo, hi, body):
        def step(i, carry):
            body(i)
            return carry

        lax.fori_loop(lo, hi, step, 0)

    each(1, ctx, lambda i: dh_copy(i).start())

    my_q = me * part_rows // piece
    def hv_wait(slot):
        chip, grp = slot // groups, lax.rem(slot, groups)
        col = lax.rem(me * part_rows + grp * piece, heads)
        source = 2 * chip + col // hloc

        @pl.when(source != me)
        def _():
            recv(hvrecv.at[slot], hv_rsem.at[slot])

    each(0, chips * groups, hv_wait)

    def dh_wait(i):
        n = lax.rem(me + i, ctx)
        recv(dhrecv.at[n], dh_rsem.at[n])

    each(1, ctx, dh_wait)

    damp = damp_ref[0, 0]
    hv_sum = hvrecv[0:groups]
    for i in range(1, chips):
        hv_sum = hv_sum + hvrecv[i * groups:(i + 1) * groups]
    hv_sum = hv_sum.reshape(part_rows, LANES)
    dh_sum = jnp.sum(jnp.sum(dhrecv[...], axis=0), keepdims=True)
    step_len = old_norm / (dir_norm + dh_sum / damp)
    dir_part = dir_ref[me]
    curved = dir_part + hv_sum / damp
    nsol = sol_ref[me] + step_len * dir_part
    nres = res_ref[me] - step_len * curved
    nsol_ref[...] = nsol
    nres_ref[...] = nres
    sq = nres * nres
    tile = nrsend.shape[0]
    if part_rows > tile:
        sq = jnp.sum(sq.reshape(part_rows // tile, tile, LANES), axis=0)
    nrsend[...] = sq
    nrrecv[me] = sq
    solrecv[me_t] = nsol

    def nr_copy(i):
        return rc(nrsend, nrrecv.at[me], nr_ssem.at[i], nr_rsem.at[me], lax.rem(me + i, ctx))

    def sol_copy(i, slot):
        return pltpu.make_async_remote_copy(
            src_ref=nsol_ref, dst_ref=solrecv.at[slot], send_sem=sol_ssem.at[i], recv_sem=sol_rsem.at[slot],
            device_id=(lax.rem(me_t + i, tasks), me), device_id_type=MESH,
        )

    for i in range(1, tasks):
        sol_copy(i, me_t).start()
    each(1, ctx, lambda i: nr_copy(i).start())

    def drain(copies):
        for copy in copies:
            copy.wait_send()

    drain(sib_copies)
    pl.when(go2)(lambda: drain(ahead2))
    pl.when(go1)(lambda: drain(ahead1))
    for d, h, copy in seg_copies:
        ok = (c + d < chips) if d else (k != h)
        pl.when(ok)(copy.wait_send)
    pl.when((c >= 2) & (odd == 1))(lambda: drain(relay1))
    pl.when((c >= 1) & go2)(lambda: drain(relay3))

    def hv_drain(i):
        r, q, owner, slot, copy = hv_copy(i)
        pl.when(owner != me)(copy.wait_send)

    each(0, rank * nq, hv_drain)
    each(1, ctx, lambda i: dh_copy(i).wait_send())

    def nr_wait(i):
        n = lax.rem(me + i, ctx)
        recv(nrrecv.at[n], nr_rsem.at[n])

    each(1, ctx, nr_wait)
    ratio = jnp.sum(jnp.sum(nrrecv[...], axis=0), keepdims=True) / old_norm
    ndir_ref[...] = nres + ratio * dir_part
    for i in range(1, tasks):
        n = lax.rem(me_t + i, tasks)
        sol_copy(i, n).wait_recv()
    meta_ref[...] = jnp.sum(solrecv[...], axis=0) / tasks
    each(1, ctx, lambda i: nr_copy(i).wait_send())
    for i in range(1, tasks):
        sol_copy(i, me_t).wait_send()


def per_device(
    tasks, ctx,
    base_queries, adapter_input, adapter_up_weight, projected_keys, projected_values,
    output_gradient, segments, solution, residual, direction, damping,
):
    tok, features = base_queries.shape[1:]
    rank = adapter_input.shape[2]
    heads = features // HEAD_DIM
    params = direction.shape[1]
    part_rows = params // ctx // LANES
    hloc = heads // 2
    piece = min(part_rows, hloc)
    nq = hloc // piece
    chips = ctx // 2
    per = heads // KV_HEADS
    kvloc = KV_HEADS // 2
    khalf = projected_keys.shape[2] // 2
    half = features // 2
    nwin = SPAN + 2
    win = SPAN + 1
    slots = chips * (part_rows // piece)
    tile = min(8, part_rows)
    f32, bf16 = jnp.float32, jnp.bfloat16
    dma = pltpu.SemaphoreType.DMA
    vmem = pl.BlockSpec(memory_space=pltpu.VMEM)
    smem = pl.BlockSpec(memory_space=pltpu.SMEM)
    out = jax.ShapeDtypeStruct((part_rows, LANES), f32)
    dims = (tasks, ctx, rank, heads, part_rows, piece, nq)
    flat = (ctx, part_rows, LANES)
    stacked = (2, kvloc, nwin, tok, per * tok)
    outs = pl.pallas_call(
        functools.partial(kernel, dims),
        out_shape=[out] * 4,
        in_specs=[vmem] * 11 + [smem],
        out_specs=[vmem] * 4,
        scratch_shapes=[
            pltpu.VMEM((nwin, tok, khalf), bf16),
            pltpu.VMEM((nwin, tok, khalf), bf16),
            pltpu.VMEM((nwin, 1, tok), jnp.int32),
            pltpu.VMEM((2, tok, half), bf16),
            pltpu.VMEM((2, tok, half), bf16),
            pltpu.VMEM((2, tok, rank), bf16),
            pltpu.VMEM((2, kvloc, per * tok, HEAD_DIM), bf16),
            pltpu.VMEM((2, kvloc, per * tok, HEAD_DIM), bf16),
            pltpu.VMEM((2, kvloc, per * tok, HEAD_DIM), bf16),
            pltpu.VMEM((hloc, rank, LANES), f32),
            pltpu.VMEM(stacked, f32),
            pltpu.VMEM(stacked, f32),
            pltpu.VMEM(stacked, f32),
            pltpu.VMEM((2, kvloc, 8, per * tok), f32),
            pltpu.VMEM((2, kvloc, win, tok, per * tok), bf16),
            pltpu.VMEM((kvloc, per * rank, LANES), f32),
            pltpu.VMEM((rank, nq, piece, LANES), f32),
            pltpu.VMEM((slots, piece, LANES), f32),
            pltpu.VMEM((8, LANES), f32),
            pltpu.VMEM((ctx, 8, LANES), f32),
            pltpu.VMEM((tile, LANES), f32),
            pltpu.VMEM((ctx, tile, LANES), f32),
            pltpu.VMEM((tasks, part_rows, LANES), f32),
            dma((8,)), dma((5,)), dma((3,)), dma((8,)), dma((nwin,)), dma((nwin,)), dma((nwin,)), dma((8,)),
            dma((rank * nq,)), dma((slots,)), dma((ctx,)), dma((ctx,)), dma((ctx,)), dma((ctx,)),
            dma((tasks,)), dma((tasks,)),
        ],
        compiler_params=pltpu.CompilerParams(
            collective_id=0, has_side_effects=True, vmem_limit_bytes=60 * 1024 * 1024
        ),
    )(
        base_queries[0], adapter_input[0], adapter_up_weight[0], projected_keys[0], projected_values[0],
        output_gradient[0], segments, solution.reshape(flat), residual.reshape(flat), direction.reshape(flat),
        direction.reshape(rank, heads, LANES), damping.reshape(1, 1),
    )
    nsol, nres, ndir, meta = outs
    return nsol.reshape(1, -1), nres.reshape(1, -1), ndir.reshape(1, -1), meta.reshape(-1)


def solution(mesh):
    in_specs = (
        P("task", "ctx", None), P("task", "ctx", None), P("task", None, None), P("task", "ctx", None),
        P("task", "ctx", None), P("task", "ctx", None), P("task", "ctx"), P("task", None), P("task", None),
        P("task", None), P("task"),
    )
    out_specs = (P("task", "ctx"), P("task", "ctx"), P("task", "ctx"), P("ctx"))
    return jax.shard_map(
        functools.partial(per_device, mesh.shape["task"], mesh.shape["ctx"]),
        mesh=mesh, in_specs=in_specs, out_specs=out_specs, check_vma=False,
    )
```

time: 249 us -> 52 us (0.21)
  waiting for transfers between devices: 96.5 us -> 0 us
  matrix products: 66.2 us -> 0 us
  starting transfers between devices: 50.8 us -> 0 us
  Pallas kernels: 0 us -> 45.5 us
  between operations: 18.1 us -> 1.31 us
  other arithmetic: 6.81 us -> 0 us
  blocking collectives: 5 us -> 0 us
    psum x1 -> x0, waiting for transfers between devices: 95.8 us -> none  [per_device(): complete_curvature_product = lax.psum(curvature_product_term, 'ctx')]
    ppermute x18 -> x0, starting transfers between devices: 50.8 us -> none  [passed_along(): lax.ppermute(value, axis, [(source, source + steps) for source in range(l...]
    pallas_call x0 -> x1, Pallas kernels: none -> 45.5 us  [per_device(): pl.pallas_call(functools.partial(kernel, dims), out_shape=[out] * 4, in_s...]
    sub x12 -> x0, matrix products: 45 us -> none  [the longest x8 35.7 us: attend(): centred = (slopes - mean_slope) * (pulls - mean_pull)]
    dot_general x11 -> x0, matrix products: 21.1 us -> none  [the longest x4 13.3 us: attend(): jnp.einsum('tgk,kd->tgd', coef_rounded, key_head, preferred_element_type=...]
    psum x1 -> x0, blocking collectives: 5 us -> none  [per_device(): meta_gradient = lax.psum(new_solution, 'task') / lax.axis_size('task')]
    reduce_sum x3 -> x0, other arithmetic: 3.73 us -> none  [the longest x1 1.55 us: per_device(): ratio = jnp.sum(res_next * res_next) / old_norm]
  transfers between devices with their start and end apart: 19 -> 0, of which waited for: 2 -> 0; matrix products, arithmetic and copies ran while one was open for 3% -> 0% of each run, Pallas kernels for 0% -> 0%
where the time goes in v1:
time: 52 us; the launch traced here: 51.6 us
  Pallas kernels  45.5 us (88%)
  local copies, waits for them, and re-layouts  4.78 us (9%)
  between operations  1.31 us (3%)
    pallas_call x1, Pallas kernels, per_device(): pl.pallas_call(functools.partial(kernel, dims), out_shape=[out] * 4, in_s...  45.5 us
    unnamed x15, local copies, waits for them, and re-layouts  4.78 us

profile of v1, /device:TPU:0, one launch (start us, length us, event | category | flops | bytes accessed | tf_op | source)
XLA Modules:
  0.0 51.6 jit_solution(468871020901763963)
XLA Ops:
  1.3 0.0 copy-start.4
  1.3 0.7 %copy-done.4 = bf16[1,128,16]{1,2,0:T(8,128)(2,1)S(1)} copy-done((bf16[1,128,16]{1,2,0:T(8,128)(2,1)S(1)}, bf16[1,128,16]{1,2,0:T(8,128)(2,1)}, u32[]{:S(2)}) %copy-start.4) | copy-done | bytes 4120
  2.0 0.7 %copy.15 = bf16[1,128,16]{2,1,0:T(8,128)(2,1)} copy(bf16[1,128,16]{1,2,0:T(8,128)(2,1)S(1)} %copy-done.4) | data formatting | bytes 8192 | tf_op args[1]
  2.7 45.5 %shard_map.138 = (f32[16,128]{1,0:T(8,128)}, f32[16,128]{1,0:T(8,128)}, f32[16,128]{1,0:T(8,128)}, f32[16,128]{1,0:T(8,128)}) custom-call(bf16[128,2048]{1,0:T(8,128)(2,1)} %bitcast.15, bf16[128,16]{1,0:T(8,128)(2,1)} %bitcast.19, bf16[16,2048]{1,0:T(8,128)(2,1)} %bitcast.24, bf16[128,512]{1,0:T(8,128)(2,1)} %bitcast.20, bf16[128,512]{1,0:T(8,128)(2,1)} %bitcast.21, ...), custom_call_target="tpu_custom_call" | custom-call | tf_op jit(solution)/shard_map/pallas_call | solution.py:437
  48.2 0.0 copy-start.3
  48.2 0.7 %copy-done.3 = f32[16,128]{1,0:T(8,128)S(1)} copy-done((f32[16,128]{1,0:T(8,128)S(1)}, f32[16,128]{1,0:T(8,128)}, u32[]{:S(2)}) %copy-start.3) | copy-done | bytes 8216
  48.9 0.0 copy-start.2
  48.9 0.6 %copy.21 = f32[1,2048]{1,0:T(1,128)} copy(f32[1,2048]{1,0:T(1,128)S(1)} %bitcast.28) | data formatting | bytes 16384
  49.5 0.1 copy-done.2
  49.6 0.0 copy-start.1
  49.6 0.6 %copy.22 = f32[1,2048]{1,0:T(1,128)} copy(f32[1,2048]{1,0:T(1,128)S(1)} %bitcast.27) | data formatting | bytes 16384
  50.2 0.1 copy-done.1
  50.3 0.0 copy-start
  50.3 0.6 %copy.23 = f32[1,2048]{1,0:T(1,128)} copy(f32[1,2048]{1,0:T(1,128)S(1)} %bitcast.26) | data formatting | bytes 16384
  50.9 0.1 copy-done
  51.0 0.6 %copy.24 = f32[2048]{0:T(1024)} copy(f32[2048]{0:T(1024)S(1)} %bitcast.25) | data formatting | bytes 16384
Async XLA Ops:
  1.3 0.7 %copy-start.4 = (bf16[1,128,16]{1,2,0:T(8,128)(2,1)S(1)}, bf16[1,128,16]{1,2,0:T(8,128)(2,1)}, u32[]{:S(2)}) copy-start(bf16[1,128,16]{1,2,0:T(8,128)(2,1)} %param.12) | copy-start | bytes 12292
  48.2 0.7 %copy-start.3 = (f32[16,128]{1,0:T(8,128)S(1)}, f32[16,128]{1,0:T(8,128)}, u32[]{:S(2)}) copy-start(f32[16,128]{1,0:T(8,128)} %get-tuple-element.8) | copy-start | bytes 24580
  48.9 0.7 %copy-start.2 = (f32[16,128]{1,0:T(8,128)S(1)}, f32[16,128]{1,0:T(8,128)}, u32[]{:S(2)}) copy-start(f32[16,128]{1,0:T(8,128)} %get-tuple-element.9) | copy-start | bytes 24580
  49.6 0.7 %copy-start.1 = (f32[16,128]{1,0:T(8,128)S(1)}, f32[16,128]{1,0:T(8,128)}, u32[]{:S(2)}) copy-start(f32[16,128]{1,0:T(8,128)} %get-tuple-element.10) | copy-start | bytes 24580
  50.3 0.7 %copy-start = (f32[16,128]{1,0:T(8,128)S(1)}, f32[16,128]{1,0:T(8,128)}, u32[]{:S(2)}) copy-start(f32[16,128]{1,0:T(8,128)} %get-tuple-element.11) | copy-start | bytes 24580

commit v2 on v1

--- a/solution.py
+++ b/solution.py
@@ -17,9 +17,10 @@
 
 def kernel(
     dims,
-    base_ref, ain_ref, up_ref, key_ref, val_ref, grad_ref, seg_ref,
+    base_hbm, ain_ref, up_ref, key_hbm, val_hbm, grad_hbm, seg_ref,
     sol_ref, res_ref, dir_ref, dirmat_ref, damp_ref,
     nsol_ref, nres_ref, ndir_ref, meta_ref,
+    base_ref, key_ref, val_ref, grad_ref, load_sem, tops, sums,
     kbuf, vbuf, segbuf, qin, gin, ain, qs, ts, gs, dsel,
     sbuf, tbuf, ubuf, mbuf, cbuf, hvacc, hvsend, hvrecv, dhsend, dhrecv,
     nrsend, nrrecv, solrecv,
@@ -29,9 +30,9 @@
     tasks, ctx, rank, heads, part_rows, piece, nq = dims
     chips = ctx // 2
     per = heads // KV_HEADS
-    tok = base_ref.shape[0]
+    tok = base_hbm.shape[0]
     half = heads * HEAD_DIM // 2
-    khalf = key_ref.shape[1] // 2
+    khalf = key_hbm.shape[1] // 2
     hloc = heads // 2
     kvloc = KV_HEADS // 2
     nwin = SPAN + 2
@@ -49,6 +50,14 @@
     def dev(n):
         return (me_t, n)
 
+    loads = [
+        pltpu.make_async_copy(src, dst, load_sem.at[i])
+        for i, (src, dst) in enumerate(
+            ((key_hbm, key_ref), (val_hbm, val_ref), (base_hbm, base_ref), (grad_hbm, grad_ref))
+        )
+    ]
+    for load in loads:
+        load.start()
     barrier = pltpu.get_barrier_semaphore()
 
     def greet(i, carry):
@@ -100,8 +109,12 @@
         for copy in copies:
             copy.start()
 
+    loads[0].wait()
+    loads[1].wait()
     pl.when(go2)(lambda: start_all(ahead2))
     pl.when(go1)(lambda: start_all(ahead1))
+    loads[2].wait()
+    loads[3].wait()
     start_all(sib_copies)
     for d, h, copy in seg_copies:
         ok = (c + d < chips) if d else (k != h)
@@ -148,7 +161,7 @@
     recv(vbuf.at[SPAN + other], v_recv.at[SPAN + other])
 
     for qb in range(2):
-        a = ain[qb]
+        a = ain[qb].astype(f32).T.astype(bf16)
         lora = jnp.dot(a, up, preferred_element_type=f32)
         tan = (
             jnp.dot(a, d1, preferred_element_type=f32)
@@ -190,6 +203,34 @@
                     tbuf[qb, h, w] = lax.dot_general(kb, ts[qb, h], NT, preferred_element_type=f32)
                     ubuf[qb, h, w] = lax.dot_general(vb, gs[qb, h], NT, preferred_element_type=f32)
 
+    factor = HEAD_DIM ** -0.5 * 1.4426950408889634
+    nblk = tok // 8
+    zero = jnp.zeros((8, tok), f32)
+
+    def fold(x):
+        return jnp.sum(x.reshape(nblk, 8, tok), axis=0)
+
+    def moments(qb, h, w, cols, top, acc):
+        e = jnp.exp2((sbuf[qb, h, w, :, cols] - top) * factor)
+        sbuf[qb, h, w, :, cols] = e
+        t = tbuf[qb, h, w, :, cols]
+        u = ubuf[qb, h, w, :, cols]
+        et = e * t
+        return (acc[0] + fold(e), acc[1] + fold(et), acc[2] + fold(e * u), acc[3] + fold(et * u))
+
+    def early_moments():
+        for qb in range(2):
+            for h in range(kvloc):
+                for g in range(per):
+                    cols = slice(g * tok, (g + 1) * tok)
+                    top = jnp.max(mbuf[qb, h, :, cols], axis=0, keepdims=True)
+                    tops[qb, h, :, cols] = jnp.broadcast_to(top, (8, tok))
+                    acc = (zero,) * 4
+                    for w in range(2, qb + win):
+                        acc = moments(qb, h, w, cols, top, acc)
+                    for i in range(4):
+                        sums[qb, h, i, :, cols] = acc[i]
+
     relay3, relay1 = [], []
     for s in range(2):
         w = SPAN - 4 + s
@@ -222,51 +263,41 @@
     arrive(1, relay3, go2)
     stage(2)
     stage(1)
+    early_moments()
     arrive(3, [], None)
     stage(3)
 
-    factor = HEAD_DIM ** -0.5 * 1.4426950408889634
-    nblk = tok // 8
     for qb in range(2):
-        at_ = ain[qb].astype(f32).T
+        at_ = ain[qb].astype(f32)
         for h in range(kvloc):
             rows_of = []
             for g in range(per):
                 cols = slice(g * tok, (g + 1) * tok)
                 top = jnp.max(mbuf[qb, h, :, cols], axis=0, keepdims=True)
-
-                def moments(w, acc, cols=cols, top=top, qb=qb, h=h):
-                    e = jnp.exp2((sbuf[qb, h, qb + w, :, cols] - top) * factor)
-                    sbuf[qb, h, qb + w, :, cols] = e
-                    t = tbuf[qb, h, qb + w, :, cols]
-                    u = ubuf[qb, h, qb + w, :, cols]
-                    et = e * t
-
-                    def fold(x):
-                        return jnp.sum(x.reshape(nblk, 8, tok), axis=0)
-
-                    return (acc[0] + fold(e), acc[1] + fold(et), acc[2] + fold(e * u), acc[3] + fold(et * u))
-
-                zero = jnp.zeros((8, tok), f32)
-                z, st, su, stu = lax.fori_loop(0, win, moments, (zero, zero, zero, zero))
-                z, st, su, stu = (jnp.sum(x, axis=0, keepdims=True) for x in (z, st, su, stu))
+                shrink = jnp.exp2((tops[qb, h, 0:1, cols] - top) * factor)
+                acc = tuple(sums[qb, h, i, :, cols] * shrink for i in range(4))
+                for w in range(qb, 2):
+                    acc = moments(qb, h, w, cols, top, acc)
+                z, st, su, stu = (jnp.sum(x, axis=0, keepdims=True) for x in acc)
                 rz = 1.0 / z
                 mt, mu = st * rz, su * rz
                 cov = stu * rz - mt * mu
-
-                def coefs(w, carry, cols=cols, mt=mt, mu=mu, cov=cov, qb=qb, h=h):
-                    e = sbuf[qb, h, qb + w, :, cols]
-                    t = tbuf[qb, h, qb + w, :, cols]
-                    u = ubuf[qb, h, qb + w, :, cols]
-                    cbuf[qb, h, w, :, cols] = (e * ((t - mt) * (u - mu) - cov)).astype(bf16)
-                    return carry
-
-                lax.fori_loop(0, win, coefs, 0)
+                covs = cov * shrink
+                for w in range(qb, qb + win):
+                    e = sbuf[qb, h, w, :, cols]
+                    t = tbuf[qb, h, w, :, cols] - mt
+                    u = ubuf[qb, h, w, :, cols] - mu
+                    inner = t * u - cov if w < 2 else t * (u * shrink) - covs
+                    cbuf[qb, h, w - qb, :, cols] = (e * inner).astype(bf16)
                 az = (at_ * rz).astype(bf16)
-                cw = cbuf[qb, h, :, :, cols].reshape(win * tok, tok)
-                rows_of.append(lax.dot_general(az, cw, NT, preferred_element_type=f32).astype(bf16))
+                blank = jnp.zeros(az.shape, bf16)
+                rows_of.append(jnp.concatenate([az if i == g else blank for i in range(per)], axis=1))
+            cw = cbuf[qb, h].reshape(win * tok, wide)
+            gw = lax.dot_general(
+                jnp.concatenate(rows_of, axis=0), cw, NT, preferred_element_type=f32
+            ).astype(bf16)
             kw = kbuf[qb:qb + win, :, h * HEAD_DIM:(h + 1) * HEAD_DIM].reshape(win * tok, HEAD_DIM)
-            hv = jnp.dot(jnp.concatenate(rows_of, axis=0), kw, preferred_element_type=f32)
+            hv = jnp.dot(gw, kw, preferred_element_type=f32)
             if qb == 0:
                 hvacc[h] = hv
             else:
@@ -430,6 +461,7 @@
     dma = pltpu.SemaphoreType.DMA
     vmem = pl.BlockSpec(memory_space=pltpu.VMEM)
     smem = pl.BlockSpec(memory_space=pltpu.SMEM)
+    hbm = pl.BlockSpec(memory_space=pl.ANY)
     out = jax.ShapeDtypeStruct((part_rows, LANES), f32)
     dims = (tasks, ctx, rank, heads, part_rows, piece, nq)
     flat = (ctx, part_rows, LANES)
@@ -437,15 +469,22 @@
     outs = pl.pallas_call(
         functools.partial(kernel, dims),
         out_shape=[out] * 4,
-        in_specs=[vmem] * 11 + [smem],
+        in_specs=[hbm, vmem, vmem, hbm, hbm, hbm] + [vmem] * 5 + [smem],
         out_specs=[vmem] * 4,
         scratch_shapes=[
+            pltpu.VMEM((tok, features), bf16),
+            pltpu.VMEM((tok, 2 * khalf), bf16),
+            pltpu.VMEM((tok, 2 * khalf), bf16),
+            pltpu.VMEM((tok, features), bf16),
+            dma((4,)),
+            pltpu.VMEM((2, kvloc, 8, per * tok), f32),
+            pltpu.VMEM((2, kvloc, 4, 8, per * tok), f32),
             pltpu.VMEM((nwin, tok, khalf), bf16),
             pltpu.VMEM((nwin, tok, khalf), bf16),
             pltpu.VMEM((nwin, 1, tok), jnp.int32),
             pltpu.VMEM((2, tok, half), bf16),
             pltpu.VMEM((2, tok, half), bf16),
-            pltpu.VMEM((2, tok, rank), bf16),
+            pltpu.VMEM((2, rank, tok), bf16),
             pltpu.VMEM((2, kvloc, per * tok, HEAD_DIM), bf16),
             pltpu.VMEM((2, kvloc, per * tok, HEAD_DIM), bf16),
             pltpu.VMEM((2, kvloc, per * tok, HEAD_DIM), bf16),
@@ -471,7 +510,7 @@
             collective_id=0, has_side_effects=True, vmem_limit_bytes=60 * 1024 * 1024
         ),
     )(
-        base_queries[0], adapter_input[0], adapter_up_weight[0], projected_keys[0], projected_values[0],
+        base_queries[0], adapter_input[0].T, adapter_up_weight[0], projected_keys[0], projected_values[0],
         output_gradient[0], segments, solution.reshape(flat), residual.reshape(flat), direction.reshape(flat),
         direction.reshape(rank, heads, LANES), damping.reshape(1, 1),
     )

time: 52 us -> 44.5 us (0.86)
  Pallas kernels: 45.5 us -> 39.4 us
  local copies, waits for them, and re-layouts: 4.78 us -> 3.39 us
    pallas_call x1, Pallas kernels: 45.5 us -> 39.4 us  [per_device(): pl.pallas_call(functools.partial(kernel, dims), out_shape=[out] * 4, in_s...]
    unnamed x15 -> x12, local copies, waits for them, and re-layouts: 4.78 us -> 3.39 us
where the time goes in v2:
time: 44.5 us; the launch traced here: 44.1 us
  Pallas kernels  39.4 us (89%)
  local copies, waits for them, and re-layouts  3.39 us (8%)
  between operations  1.3 us (3%)
    pallas_call x1, Pallas kernels, per_device(): pl.pallas_call(functools.partial(kernel, dims), out_shape=[out] * 4, in_s...  39.4 us
    unnamed x12, local copies, waits for them, and re-layouts  3.39 us

profile of v2, /device:TPU:0, one launch (start us, length us, event | category | flops | bytes accessed | tf_op | source)
XLA Modules:
  0.0 44.1 jit_solution(10199975390854128779)
XLA Ops:
  1.3 39.4 %shard_map.138 = (f32[16,128]{1,0:T(8,128)}, f32[16,128]{1,0:T(8,128)}, f32[16,128]{1,0:T(8,128)}, f32[16,128]{1,0:T(8,128)}) custom-call(bf16[128,2048]{1,0:T(8,128)(2,1)} %bitcast.17, bf16[16,128]{1,0:T(8,128)(2,1)} %bitcast.30, bf16[16,2048]{1,0:T(8,128)(2,1)} %bitcast.25, bf16[128,512]{1,0:T(8,128)(2,1)} %bitcast.21, bf16[128,512]{1,0:T(8,128)(2,1)} %bitcast.22, ...), custom_call_target="tpu_custom_call" | custom-call | tf_op jit(solution)/shard_map/pallas_call | solution.py:469
  40.7 0.0 copy-start.3
  40.7 0.7 %copy-done.3 = f32[16,128]{1,0:T(8,128)S(1)} copy-done((f32[16,128]{1,0:T(8,128)S(1)}, f32[16,128]{1,0:T(8,128)}, u32[]{:S(2)}) %copy-start.3) | copy-done | bytes 8216
  41.4 0.0 copy-start.2
  41.4 0.6 %copy.20 = f32[1,2048]{1,0:T(1,128)} copy(f32[1,2048]{1,0:T(1,128)S(1)} %bitcast.29) | data formatting | bytes 16384
  42.0 0.1 copy-done.2
  42.1 0.0 copy-start.1
  42.1 0.6 %copy.21 = f32[1,2048]{1,0:T(1,128)} copy(f32[1,2048]{1,0:T(1,128)S(1)} %bitcast.28) | data formatting | bytes 16384
  42.7 0.1 copy-done.1
  42.8 0.0 copy-start
  42.8 0.6 %copy.22 = f32[1,2048]{1,0:T(1,128)} copy(f32[1,2048]{1,0:T(1,128)S(1)} %bitcast.27) | data formatting | bytes 16384
  43.4 0.1 copy-done
  43.5 0.6 %copy.23 = f32[2048]{0:T(1024)} copy(f32[2048]{0:T(1024)S(1)} %bitcast.26) | data formatting | bytes 16384
Async XLA Ops:
  40.7 0.7 %copy-start.3 = (f32[16,128]{1,0:T(8,128)S(1)}, f32[16,128]{1,0:T(8,128)}, u32[]{:S(2)}) copy-start(f32[16,128]{1,0:T(8,128)} %get-tuple-element.8) | copy-start | bytes 24580
  41.4 0.7 %copy-start.2 = (f32[16,128]{1,0:T(8,128)S(1)}, f32[16,128]{1,0:T(8,128)}, u32[]{:S(2)}) copy-start(f32[16,128]{1,0:T(8,128)} %get-tuple-element.9) | copy-start | bytes 24580
  42.1 0.7 %copy-start.1 = (f32[16,128]{1,0:T(8,128)S(1)}, f32[16,128]{1,0:T(8,128)}, u32[]{:S(2)}) copy-start(f32[16,128]{1,0:T(8,128)} %get-tuple-element.10) | copy-start | bytes 24580
  42.8 0.7 %copy-start = (f32[16,128]{1,0:T(8,128)S(1)}, f32[16,128]{1,0:T(8,128)}, u32[]{:S(2)}) copy-start(f32[16,128]{1,0:T(8,128)} %get-tuple-element.11) | copy-start | bytes 24580
